TPU v7x, 128 devices: a whole 4x4x4 slice. The times are simulated.
128 devices in a mesh: seq: 16 (over z, y_hi, core), fsdp: 8 (over y_lo, x).
Axes of the slice: x: 4, y: 4 (y_hi: 2, y_lo: 2; y = y_hi * 2 + y_lo), z: 4, core: 2. Of those that a mesh axis runs over, the one named last changes fastest.
Arguments:
- patches: bfloat16 [8, 2048, 3072], P('fsdp', 'seq'), may hold values from -6 to 6
- weight_codes: int32 [3072, 3072], P('fsdp'), may hold values from -448 to 448
- block_scales: float32 [24, 24], P('fsdp'), may hold values from 2.5e-05 to 0.0001
- key_proj: bfloat16 [8, 2048, 3072], P('fsdp', 'seq'), may hold values from -6 to 6
- value_proj: bfloat16 [8, 2048, 3072], P('fsdp', 'seq'), may hold values from -6 to 6
- query_gain: float32 [3072], replicated, may hold values from 1 to 10
- key_gain: float32 [3072], replicated, may hold values from 1 to 10
Outputs:
- attended: bfloat16 [8, 2048, 3072], P('fsdp', 'seq')
All inputs are finite; a program needn't handle non-finite values.
Results may differ from a plain program's by a relative error of at most 0.007.
The roundings to bfloat16 on the way count: a program that leaves them out, or rounds other values in their place, can miss the bound.
Values may be sent and summed in bfloat16 or wider, within the bound.
A program may use at most 192 MiB of HBM per device.

v0:
```python
import math

import jax
import jax.numpy as jnp
from jax import lax
from jax.sharding import Mesh
from jax.sharding import PartitionSpec as P

HEADS = 48
HDIM = 64
BLOCK = 128
SEQ = ("seq_0", "seq_1", "seq_2")


NORM_FLOOR = 0.25


def split_up(array, dim, devices):
    before, after = (array.shape[:dim], array.shape[dim + 1 :])
    return jnp.moveaxis(array.reshape(*before, devices, -1, *after), dim, 0)


def laid_out(tiles, dim):
    tiles = jnp.moveaxis(tiles, 0, dim)
    lengths = tiles.shape
    return tiles.reshape(*lengths[:dim], lengths[dim] * lengths[dim + 1], *lengths[dim + 2 :])


def exchange_in_order(tiles, axes, order):
    inside = tiles.shape[1:]
    whole = tiles.reshape(*(lax.axis_size(a) for a in axes), *inside)
    for k in order:
        whole = lax.all_to_all(whole, axes[k], k, k, tiled=True)
    return whole.reshape(-1, *inside)


def two_step_exchange(array, groups, order, split_dim, concat_dim):
    devices = lax.axis_size(groups[0]) * lax.axis_size(groups[1])
    tiles = split_up(array, split_dim, devices)
    return laid_out(exchange_in_order(tiles, groups, order), concat_dim)


def head_norm(projected, gain_row):
    shaped = projected.reshape(projected.shape[:-1] + (HEADS, HDIM))
    average = jnp.mean(shaped, axis=-1, keepdims=True)
    centred = shaped - average
    spread = jnp.mean(centred * centred, axis=-1, keepdims=True)
    normed = centred * lax.rsqrt(spread + NORM_FLOOR) * gain_row.reshape(HEADS, HDIM)
    return normed.astype(jnp.bfloat16)


def dequantize(weight_codes, block_scales):
    row_count, column_count = weight_codes.shape
    blocked = weight_codes.astype(jnp.float32).reshape(
        row_count // BLOCK, BLOCK, column_count // BLOCK, BLOCK
    )
    return (
        (blocked * block_scales[:, None, :, None])
        .reshape(row_count, column_count)
        .astype(jnp.bfloat16)
    )


def start_of(query_view):
    image_count, token_count, head_count = (
        query_view.shape[0],
        query_view.shape[1],
        query_view.shape[2],
    )
    return (
        jnp.full((image_count, token_count, head_count), -1e30, jnp.float32),
        jnp.zeros((image_count, token_count, head_count), jnp.float32),
        jnp.zeros(query_view.shape, jnp.float32),
    )


def attend_block(query_view, state_now, key_view, value_view):
    running_max, running_sum, weighted = state_now
    scores = jnp.einsum(
        "ithd,ishd->iths", query_view, key_view, preferred_element_type=jnp.float32
    ) * HDIM ** (-0.5)
    newest = jnp.maximum(running_max, jnp.max(scores, axis=-1))
    probability = jnp.exp(scores - newest[..., None])
    running_sum = jnp.sum(probability, axis=-1)
    blended = jnp.einsum(
        "iths,ishd->ithd",
        probability.astype(jnp.bfloat16),
        value_view,
        preferred_element_type=jnp.float32,
    )
    weighted = blended
    return (newest, running_sum, weighted)


def attend_whole(members):
    query_all, key_all, value_all = members
    image_count, length, head_count, head_size = query_all.shape
    block_rows = math.gcd(length, 512)
    block_count = length // block_rows
    blocked = jnp.moveaxis(
        query_all.reshape(image_count, block_count, block_rows, head_count, head_size), 1, 0
    )

    def one_block(query_block):
        finished = attend_block(query_block, start_of(query_block), key_all, value_all)
        return (finished[2] / finished[1][..., None]).astype(jnp.bfloat16)

    outputs = lax.map(one_block, blocked)
    return jnp.moveaxis(outputs, 0, 1).reshape(image_count, length, head_count, head_size)


def per_device(patches, weight_codes, block_scales, key_proj, value_proj, query_gain, key_gain):
    image_count, token_count, feature_count = patches.shape
    flat_rows = patches.reshape(image_count * token_count, feature_count)
    key_norm = head_norm(key_proj.astype(jnp.float32), key_gain)
    value_view = value_proj.reshape(image_count, token_count, HEADS, HDIM)
    local_weight = dequantize(weight_codes, block_scales)
    group_rows = lax.all_to_all(flat_rows, "fsdp", split_axis=1, concat_axis=0, tiled=True)
    queries = lax.psum_scatter(
        jnp.dot(group_rows, local_weight, preferred_element_type=jnp.float32),
        "fsdp",
        scatter_dimension=0,
        tiled=True,
    )
    query_view = head_norm(queries, query_gain).reshape(image_count, token_count, HEADS, HDIM)
    mixed = attend_whole(
        (
            lax.all_to_all(query_view, SEQ, split_axis=2, concat_axis=1, tiled=True),
            lax.all_to_all(key_norm, SEQ, split_axis=2, concat_axis=1, tiled=True),
            lax.all_to_all(value_view, SEQ, split_axis=2, concat_axis=1, tiled=True),
        )
    )
    back = two_step_exchange(mixed, (("seq_0", "seq_1"), "seq_2"), (1, 0), 1, 2)
    return back.reshape(image_count, token_count, HEADS * HDIM)


def solution(mesh):
    split = Mesh(
        mesh.devices.reshape(4, 2, 2, mesh.shape["fsdp"]), ("seq_0", "seq_1", "seq_2", "fsdp")
    )
    placed = (
        P("fsdp", SEQ, None),
        P("fsdp", None),
        P("fsdp", None),
        P("fsdp", SEQ, None),
        P("fsdp", SEQ, None),
        P(),
        P(),
    )
    return jax.shard_map(
        per_device, mesh=split, in_specs=placed, out_specs=P("fsdp", SEQ, None), check_vma=False
    )
```

profile of v0, /device:TPU:1, one launch (start us, length us, event | category | flops | bytes accessed | tf_op | source)
XLA Modules:
  0.0 281.7 jit_solution(18361344485200395477)
XLA Ops:
  6.5 1.5 copy.27
  8.1 17.7 %all_to_all.80 = bf16[128,8,384]{0,2,1:T(8,128)(2,1)S(1)} all-to-all(bf16[128,8,384]{0,2,1:T(8,128)(2,1)S(1)} %bitcast.155), channel_id=1, replica_groups=mesh['seq_0'=4,'seq_1'=2,'seq_2'=2,'fsdp'=8] {'fsdp'}, dimensions={1} | all-to-all | bytes 1572864 | tf_op jit(solution)/shard_map/all_to_all | solution.py:118
  25.7 0.4 copy.28
  26.1 0.4 mul.106
  26.5 2.0 copy-done.1
  28.5 7.1 %convolution_bitcast_fusion = f32[1024,3072]{0,1:T(8,128)} fusion(bf16[1024,384]{1,0:T(8,128)(2,1)S(1)} %bitcast.148, f32[48,8,24,128]{3,2,1,0:T(8,128)S(1)} %bitcast.144, s32[384,3072]{1,0:T(8,128)S(1)} %copy-done.1), kind=kOutput, calls=%fused_computation.20 | convolution fusion | flops 2419458048 | bytes 22806528 | tf_op jit(solution)/shard_map/dot_general | solution.py:120
  35.6 1.1 copy-done.2
  36.7 0.4 copy.31
  37.1 0.1 convert_element_type.39
  37.3 0.2 reduce_sum.47
  37.5 0.3 multiply_reduce_fusion
  37.8 1.4 fusion.30
  39.1 9.5 %all-to-all-start.2 = ((bf16[1,128,48,64]{1,3,0,2:T(8,128)(2,1)}), bf16[1,128,48,64]{1,3,0,2:T(8,128)(2,1)S(1)}, u32[]{:S(2)}, u32[]{:S(2)}) async-start(bf16[1,128,48,64]{1,3,0,2:T(8,128)(2,1)} %fusion.30), calls=%async_computation.3 | async-start | bytes 1572864 | tf_op jit(solution)/shard_map/all_to_all | solution.py:129
  48.7 1.1 copy.34
  49.8 119.5 %reduce-scatter.2.cloned.1.call-done = f32[128,3072]{0,1:T(8,128)} async-done(((f32[1024,3072]{0,1:T(8,128)}), f32[128,3072]{0,1:T(8,128)}) %reduce-scatter.2.cloned.1.call-update) | async-done | bytes 1572880 | tf_op jit(solution)/shard_map/reduce_scatter | solution.py:119
  169.3 1.7 reduce_sum.45
  171.0 9.2 %all-to-all-done.2 = bf16[1,128,48,64]{1,3,0,2:T(8,128)(2,1)S(1)} async-done(((bf16[1,128,48,64]{1,3,0,2:T(8,128)(2,1)}), bf16[1,128,48,64]{1,3,0,2:T(8,128)(2,1)S(1)}, u32[]{:S(2)}, u32[]{:S(2)}) %all-to-all-start.2) | async-done | bytes 786464 | tf_op jit(solution)/shard_map/all_to_all | solution.py:129
  180.2 3.9 %all-to-all-start.3 = ((bf16[1,128,48,64]{1,3,0,2:T(8,128)(2,1)}), bf16[1,128,48,64]{1,3,0,2:T(8,128)(2,1)S(1)}, u32[]{:S(2)}, u32[]{:S(2)}) async-start(bf16[1,128,48,64]{1,3,0,2:T(8,128)(2,1)} %bitcast.151), calls=%async_computation.4 | async-start | bytes 1572864 | tf_op jit(solution)/shard_map/all_to_all | solution.py:130
  184.1 1.7 multiply_reduce_fusion.1
  185.8 1.4 multiply_convert_fusion.1
  187.2 10.9 %all-to-all-done.3 = bf16[1,128,48,64]{1,3,0,2:T(8,128)(2,1)S(1)} async-done(((bf16[1,128,48,64]{1,3,0,2:T(8,128)(2,1)}), bf16[1,128,48,64]{1,3,0,2:T(8,128)(2,1)S(1)}, u32[]{:S(2)}, u32[]{:S(2)}) %all-to-all-start.3) | async-done | bytes 786464 | tf_op jit(solution)/shard_map/all_to_all | solution.py:130
  198.1 4.7 %all-to-all-start.1 = ((bf16[1,128,48,64]{1,3,0,2:T(8,128)(2,1)}), bf16[1,128,48,64]{1,3,0,2:T(8,128)(2,1)S(1)}, u32[]{:S(2)}, u32[]{:S(2)}) async-start(bf16[1,128,48,64]{1,3,0,2:T(8,128)(2,1)} %multiply_convert_fusion.1), calls=%async_computation.2 | async-start | bytes 1572864 | tf_op jit(solution)/shard_map/all_to_all | solution.py:128
  202.8 0.2 copy.51
  203.0 1.1 copy.50
  204.1 12.8 %all-to-all-done.1 = bf16[1,128,48,64]{1,3,0,2:T(8,128)(2,1)S(1)} async-done(((bf16[1,128,48,64]{1,3,0,2:T(8,128)(2,1)}), bf16[1,128,48,64]{1,3,0,2:T(8,128)(2,1)S(1)}, u32[]{:S(2)}, u32[]{:S(2)}) %all-to-all-start.1) | async-done | bytes 786464 | tf_op jit(solution)/shard_map/all_to_all | solution.py:128
  216.9 0.5 copy.30
  217.4 0.3 transpose_reshape.3
  217.7 0.2 copy.37
  217.8 30.9 %while.10 = (s32[]{:T(128)}, bf16[4,1,512,3,64]{2,4,3,1,0:T(8,128)(2,1)}, bf16[4,1,512,3,64]{2,4,3,1,0:T(8,128)(2,1)S(1)}, bf16[1,2048,3,64]{1,3,2,0:T(8,128)(2,...) while((s32[]{:T(128)}, bf16[4,1,512,3,64]{2,4,3,1,0:T(8,128)(2,1)}, ...), condition=%wide.region_8.9_spmd, body=%wide.region_5.8_spmd.sunk | while | flops 830667264 | bytes 42904164 | solution.py:108
  217.8 1.9 bitcast_reduce_fusion.2
  219.8 2.5 fusion.38
  222.3 3.3 %fusion.39 = bf16[4,1,512,3,64]{2,4,3,1,0:T(8,128)(2,1)} fusion(bf16[4,1,512,3,64]{2,4,3,1,0:T(8,128)(2,1)} %get-tuple-element.102, s32[]{:T(128)} %get-tuple-element.101, f32[3,512,2048]{2,1,0:T(8,128)S(1)} %get-tuple-element.93, f32[512,3]{0,1:T(4,128)S(1)} %broadcast_maximum_fusion.2, bf16[1,2048,3,64]{1,3,2,0:T(8,128)(2,1)S(1)} %copy-done.4, ...), kind=kOutput, calls=%fused_computation.11.clone.1 | convolution fusion | flops 412286976 | bytes 13578752 | tf_op jit(solution)/shard_map/while/body/eval_jaxpr/iths,ishd->ithd/dot_general | solution.py:85
  225.6 1.9 bitcast_reduce_fusion.2
  227.5 2.5 fusion.38
  230.0 3.3 %fusion.39 = bf16[4,1,512,3,64]{2,4,3,1,0:T(8,128)(2,1)} fusion(bf16[4,1,512,3,64]{2,4,3,1,0:T(8,128)(2,1)} %get-tuple-element.102, s32[]{:T(128)} %get-tuple-element.101, f32[3,512,2048]{2,1,0:T(8,128)S(1)} %get-tuple-element.93, f32[512,3]{0,1:T(4,128)S(1)} %broadcast_maximum_fusion.2, bf16[1,2048,3,64]{1,3,2,0:T(8,128)(2,1)S(1)} %copy-done.4, ...), kind=kOutput, calls=%fused_computation.11.clone.1 | convolution fusion | flops 412286976 | bytes 13578752 | tf_op jit(solution)/shard_map/while/body/eval_jaxpr/iths,ishd->ithd/dot_general | solution.py:85
  233.3 1.9 bitcast_reduce_fusion.2
  235.2 2.5 fusion.38
  237.7 3.3 %fusion.39 = bf16[4,1,512,3,64]{2,4,3,1,0:T(8,128)(2,1)} fusion(bf16[4,1,512,3,64]{2,4,3,1,0:T(8,128)(2,1)} %get-tuple-element.102, s32[]{:T(128)} %get-tuple-element.101, f32[3,512,2048]{2,1,0:T(8,128)S(1)} %get-tuple-element.93, f32[512,3]{0,1:T(4,128)S(1)} %broadcast_maximum_fusion.2, bf16[1,2048,3,64]{1,3,2,0:T(8,128)(2,1)S(1)} %copy-done.4, ...), kind=kOutput, calls=%fused_computation.11.clone.1 | convolution fusion | flops 412286976 | bytes 13578752 | tf_op jit(solution)/shard_map/while/body/eval_jaxpr/iths,ishd->ithd/dot_general | solution.py:85
  241.0 1.9 bitcast_reduce_fusion.2
  243.0 2.5 fusion.38
  245.4 3.3 %fusion.39 = bf16[4,1,512,3,64]{2,4,3,1,0:T(8,128)(2,1)} fusion(bf16[4,1,512,3,64]{2,4,3,1,0:T(8,128)(2,1)} %get-tuple-element.102, s32[]{:T(128)} %get-tuple-element.101, f32[3,512,2048]{2,1,0:T(8,128)S(1)} %get-tuple-element.93, f32[512,3]{0,1:T(4,128)S(1)} %broadcast_maximum_fusion.2, bf16[1,2048,3,64]{1,3,2,0:T(8,128)(2,1)S(1)} %copy-done.4, ...), kind=kOutput, calls=%fused_computation.11.clone.1 | convolution fusion | flops 412286976 | bytes 13578752 | tf_op jit(solution)/shard_map/while/body/eval_jaxpr/iths,ishd->ithd/dot_general | solution.py:85
  248.7 1.7 copy.38
  250.5 0.3 reshape_transpose_reshape_reshape_transpose.3
  250.9 5.2 %all_to_all.81 = bf16[8,2,1,128,3,64]{3,0,5,4,2,1:T(8,128)(2,1)S(1)} all-to-all(bf16[8,2,1,128,3,64]{3,0,5,4,2,1:T(8,128)(2,1)S(1)} %copy.39), channel_id=1, replica_groups=mesh['seq_0'=4,'seq_1'=2,'seq_2'=2,'fsdp'=8] {'seq_2'}, dimensions={1} | all-to-all | bytes 1572864 | tf_op jit(solution)/shard_map/all_to_all | solution.py:33
  256.1 0.8 copy.40
  257.0 16.5 %all_to_all.82 = bf16[8,2,1,128,3,64]{3,1,5,4,2,0:T(2,128)(2,1)S(1)} all-to-all(bf16[8,2,1,128,3,64]{3,1,5,4,2,0:T(2,128)(2,1)S(1)} %copy.40), channel_id=1, replica_groups=mesh['seq_0'=4,'seq_1'=2,'seq_2'=2,'fsdp'=8] {'seq_0','seq_1'}, dimensions={0} | all-to-all | bytes 1572864 | tf_op jit(solution)/shard_map/all_to_all | solution.py:33
  273.5 0.2 copy.41
  273.7 1.2 copy.42
  (34 shorter events, 0.4 us)
Async XLA Ops:
  6.5 19.6 %copy-start.7 = (f32[3,24]{1,0:T(4,128)S(1)}, f32[3,24]{1,0:T(4,128)}, u32[]{:S(2)}) copy-start(f32[3,24]{1,0:T(4,128)} %param.11) | copy-start | bytes 868
  6.5 162.8 %reduce-scatter.2.cloned.1.call-start = ((), (), s32[]{:S(2)}) async-start(), calls=%async_computation.7 | async-start | bytes 14155776 | tf_op jit(solution)/shard_map/reduce_scatter | solution.py:119
  26.1 2.3 copy-start.1
  35.5 1.1 copy-start.2
  35.6 1.6 copy-start.5
  37.1 11.6 %copy-start.6 = (f32[3072]{0:T(1024)S(1)}, f32[3072]{0:T(1024)}, u32[]{:S(2)}) copy-start(f32[3072]{0:T(1024)} %param.14) | copy-start | bytes 36868
  37.1 11.6 %copy-start.3 = (bf16[1,128,3072]{2,1,0:T(8,128)(2,1)S(1)}, bf16[1,128,3072]{2,1,0:T(8,128)(2,1)}, u32[]{:S(2)}) copy-start(bf16[1,128,3072]{2,1,0:T(8,128)(2,1)} %param.13) | copy-start | bytes 2359300
  39.1 141.1 %all-to-all-start.2 = ((bf16[1,128,48,64]{1,3,0,2:T(8,128)(2,1)}), bf16[1,128,48,64]{1,3,0,2:T(8,128)(2,1)S(1)}, u32[]{:S(2)}, u32[]{:S(2)}) async-start(bf16[1,128,48,64]{1,3,0,2:T(8,128)(2,1)} %fusion.30), calls=%async_computation.3 | async-start | bytes 1572864 | tf_op jit(solution)/shard_map/all_to_all | solution.py:129
  169.3 16.5 %copy-start = (f32[128,3072]{0,1:T(8,128)S(1)}, f32[128,3072]{0,1:T(8,128)}, u32[]{:S(2)}) copy-start(f32[128,3072]{0,1:T(8,128)} %reduce-scatter.2.cloned.1.call-done) | copy-start | bytes 4718596
  180.2 17.9 %all-to-all-start.3 = ((bf16[1,128,48,64]{1,3,0,2:T(8,128)(2,1)}), bf16[1,128,48,64]{1,3,0,2:T(8,128)(2,1)S(1)}, u32[]{:S(2)}, u32[]{:S(2)}) async-start(bf16[1,128,48,64]{1,3,0,2:T(8,128)(2,1)} %bitcast.151), calls=%async_computation.4 | async-start | bytes 1572864 | tf_op jit(solution)/shard_map/all_to_all | solution.py:130
  198.1 18.7 %all-to-all-start.1 = ((bf16[1,128,48,64]{1,3,0,2:T(8,128)(2,1)}), bf16[1,128,48,64]{1,3,0,2:T(8,128)(2,1)S(1)}, u32[]{:S(2)}, u32[]{:S(2)}) async-start(bf16[1,128,48,64]{1,3,0,2:T(8,128)(2,1)} %multiply_convert_fusion.1), calls=%async_computation.2 | async-start | bytes 1572864 | tf_op jit(solution)/shard_map/all_to_all | solution.py:128
  219.8 2.5 copy-start.4
  227.5 2.5 copy-start.4
  235.2 2.5 copy-start.4
  242.9 2.5 copy-start.4
Sparse Core Ops, SparseCore 0:
  35.7 133.5 reduce-scatter.1
where the time goes:
time: 282 us
  waiting for transfers between devices  152 us (54%)
  blocking collectives  39.5 us (14%)
  matrix products  28 us (10%)
  starting transfers between devices  18 us (6%)
  other arithmetic  16.6 us (6%)
  local copies, waits for them, and re-layouts  13.6 us (5%)
  between operations  13.6 us (5%)
    reduce_scatter x1, waiting for transfers between devices, per_device(): lax.psum_scatter(jnp.dot(group_rows, local_weight, preferred_element_type...  119 us
    all_to_all x2, blocking collectives, exchange_in_order(): whole = lax.all_to_all(whole, axes[k], k, k, tiled=True)  21.8 us
    all_to_all x1, blocking collectives, per_device(): lax.all_to_all(flat_rows, 'fsdp', split_axis=1, concat_axis=0, tiled=True)  17.7 us
    dot_general x4, matrix products, attend_block(): jnp.einsum('iths,ishd->ithd', probability.astype(jnp.bfloat16), value_vie...  13.2 us
    all_to_all x1, waiting for transfers between devices, per_device(): lax.all_to_all(query_view, SEQ, split_axis=2, concat_axis=1, tiled=True)  12.8 us
    all_to_all x1, waiting for transfers between devices, per_device(): lax.all_to_all(value_view, SEQ, split_axis=2, concat_axis=1, tiled=True)  10.9 us
    reduce_sum x4, other arithmetic, attend_block(): running_sum = jnp.sum(probability, axis=-1)  9.85 us
    all_to_all x1, starting transfers between devices, per_device(): lax.all_to_all(key_norm, SEQ, split_axis=2, concat_axis=1, tiled=True)  9.47 us
  transfers between devices with their start and end apart: 4, of which 4 were waited for; matrix products, arithmetic and copies ran while one was open for 3% of the time, Pallas kernels for 0%

commit v1 on v0

v1 whole, which is shorter than its diff:
```python
import jax
import jax.numpy as jnp
from jax import lax
from jax.experimental import pallas as pl
from jax.experimental.pallas import tpu as pltpu
from jax.sharding import Mesh
from jax.sharding import PartitionSpec as P

HDIM = 64
BLOCK = 128
NORM_FLOOR = 0.25
AXES = ("z", "yh", "c", "yl", "x")
MESH = pl.DeviceIdType.MESH

TOKENS = 128
FEATURES = 3072
ROWS = 384
PAIRS = 3
COLS = PAIRS * BLOCK
HALF = TOKENS // 2

KV_ROUTES = ((0, 1), (1, 0), (1, 1), (3, 0), (3, 1), (2, 0), (2, 1))
X_ROUTES = (1, 3, 2)


def split_dot(values, ones):
    high = values.astype(jnp.bfloat16)
    low = (values - high.astype(jnp.float32)).astype(jnp.bfloat16)
    return jnp.dot(high, ones, preferred_element_type=jnp.float32) + jnp.dot(
        low, ones, preferred_element_type=jnp.float32
    )


def head_ones():
    row = lax.broadcasted_iota(jnp.int32, (BLOCK, BLOCK), 0) // HDIM
    column = lax.broadcasted_iota(jnp.int32, (BLOCK, BLOCK), 1) // HDIM
    return jnp.where(row == column, 1.0, 0.0).astype(jnp.bfloat16)


def pair_norm(values, total, gain_row, ones):
    centred = values - total * (1.0 / HDIM)
    spread = split_dot(centred * centred, ones) * (1.0 / HDIM)
    return centred * lax.rsqrt(spread + NORM_FLOOR) * gain_row


def kernel(
    patches, codes, scales, keys, values, query_gain, key_gain, out,
    patch_all, weight_all, own_kv, kv_all, code_block, query_all, attended,
    local_sem, w_send, w_recv, kv_send, kv_recv, y_send, y_recv, p_send, p_recv, o_send, o_recv, o_local,
):
    z, yh, c = lax.axis_index("z"), lax.axis_index("yh"), lax.axis_index("c")
    yl, x = lax.axis_index("yl"), lax.axis_index("x")
    y = yh * 2 + yl

    def at(dz=0, dy=0, dx=0, dc=0):
        row = lax.rem(y + dy, 4)
        return (
            lax.rem(z + dz, 4), lax.div(row, 2), lax.rem(c + dc, 2), lax.rem(row, 2), lax.rem(x + dx, 4),
        )

    def remote(source, target, send, recv, device):
        return pltpu.make_async_remote_copy(
            src_ref=source, dst_ref=target, send_sem=send, recv_sem=recv, device_id=device, device_id_type=MESH,
        )

    own = z * 2 + c
    chunk = yl * 4 + x
    other_chunk = (1 - yl) * 4 + x
    first_column = pl.multiple_of(own * COLS, BLOCK)

    barrier = pltpu.get_barrier_semaphore()
    partners = [at(dz=dz, dc=dc) for dz, dc in KV_ROUTES]
    partners += [at(dy=dy) for dy in (1, 2, 3)] + [at(dx=dx) for dx in X_ROUTES]
    for partner in partners:
        pl.semaphore_signal(barrier, inc=1, device_id=partner, device_id_type=MESH)

    load_codes = pltpu.make_async_copy(codes.at[:, pl.ds(first_column, COLS)], code_block, local_sem.at[0])
    load_keys = pltpu.make_async_copy(keys.at[0], own_kv.at[0], local_sem.at[1])
    load_values = pltpu.make_async_copy(values.at[0], own_kv.at[1], local_sem.at[2])
    load_patches = pltpu.make_async_copy(patches.at[0], patch_all.at[own], local_sem.at[3])
    for load in (load_codes, load_keys, load_values, load_patches):
        load.start()

    load_codes.wait()
    for r in range(ROWS // BLOCK):
        for k in range(PAIRS):
            block = code_block[r * BLOCK : (r + 1) * BLOCK, k * BLOCK : (k + 1) * BLOCK]
            weight_all[chunk, r * BLOCK : (r + 1) * BLOCK, k * BLOCK : (k + 1) * BLOCK] = (
                block.astype(jnp.float32) * scales[r, own * PAIRS + k]
            ).astype(jnp.bfloat16)
    pl.semaphore_wait(barrier, len(partners))

    half_rows = ROWS // 2
    weight_y = [
        remote(
            weight_all.at[chunk, pl.ds(part * half_rows, half_rows)],
            weight_all.at[chunk, pl.ds(part * half_rows, half_rows)],
            w_send.at[part], w_recv.at[part], at(dy=dy),
        )
        for part, dy in ((0, 1), (1, 3))
    ]
    weight_x = [
        remote(weight_all.at[chunk], weight_all.at[chunk], w_send.at[2 + i], w_recv.at[2 + i], at(dx=dx))
        for i, dx in enumerate(X_ROUTES)
    ]
    weight_x2 = [
        remote(
            weight_all.at[other_chunk], weight_all.at[other_chunk], w_send.at[5 + i], w_recv.at[5 + i], at(dx=dx),
        )
        for i, dx in enumerate(X_ROUTES)
    ]
    for copy in weight_y + weight_x:
        copy.start()

    ones = head_ones()
    load_keys.wait()

    def normalize_keys(k, carry):
        lanes = pl.ds(pl.multiple_of(k * BLOCK, BLOCK), BLOCK)
        block = own_kv[0, :, lanes]
        total = jnp.dot(block, ones, preferred_element_type=jnp.float32)
        own_kv[0, :, lanes] = pair_norm(
            block.astype(jnp.float32), total, key_gain[:, lanes], ones
        ).astype(jnp.bfloat16)
        return carry

    lax.fori_loop(0, FEATURES // BLOCK, normalize_keys, 0, unroll=4)
    load_values.wait()

    def kv_copy(pair, route):
        dz, dc = KV_ROUTES[route]
        target = at(dz=dz, dc=dc)
        column = pl.multiple_of((target[0] * 2 + target[2]) * COLS + pair * BLOCK, BLOCK)
        return remote(
            own_kv.at[:, :, pl.ds(column, BLOCK)], kv_all.at[pair, :, yh, own],
            kv_send.at[pair, route], kv_recv.at[pair, route], target,
        )

    def slot_of(route):
        if route == len(KV_ROUTES):
            return own
        dz, dc = KV_ROUTES[route]
        return lax.rem(z + 4 - dz, 4) * 2 + lax.rem(c + dc, 2)

    def y_copy(pair, route):
        place = kv_all.at[pair, :, yh, slot_of(route)]
        return remote(place, place, y_send.at[pair, route], y_recv.at[pair, route], at(dy=2))

    for pair in range(PAIRS):
        for route in range(len(KV_ROUTES)):
            kv_copy(pair, route).start()

    load_patches.wait()
    low, high = pl.ds(0, HALF), pl.ds(HALF, HALF)
    down, up, across = lax.rem(z + 3, 4) * 2 + c, lax.rem(z + 1, 4) * 2 + c, lax.rem(z + 2, 4) * 2 + c

    def patch_copy(which):
        slot, rows, target = (
            (own, low, at(dz=1)), (own, high, at(dz=1)), (own, high, at(dz=3)), (own, low, at(dz=3)),
            (down, low, at(dz=1)), (up, high, at(dz=3)),
            (own, None, at(dc=1)), (down, None, at(dc=1)), (up, None, at(dc=1)), (across, None, at(dc=1)),
        )[which]
        place = patch_all.at[slot] if rows is None else patch_all.at[slot, rows]
        return remote(place, place, p_send.at[which], p_recv.at[which], target)

    patch_copy(6).start()
    for which in range(4):
        patch_copy(which).start()

    for pair in range(PAIRS):
        for part in range(2):
            kv_all[pair, part, yh, own] = own_kv[
                part, :, pl.ds(pl.multiple_of(own * COLS + pair * BLOCK, BLOCK), BLOCK)
            ]

    for copy in weight_y:
        copy.wait_recv()
    for copy in weight_x2:
        copy.start()

    for pair in range(PAIRS):
        y_copy(pair, len(KV_ROUTES)).start()
        for route in range(len(KV_ROUTES)):
            kv_copy(pair, route).wait_recv()
            y_copy(pair, route).start()
    patch_copy(0).wait_recv()
    patch_copy(4).start()
    patch_copy(2).wait_recv()
    patch_copy(5).start()
    for copy in weight_x + weight_x2:
        copy.wait_recv()

    def out_copy(step, chip, pair, dc):
        target = (chip, yh, lax.rem(c + dc, 2), yl, x)
        lanes = pl.ds(pl.multiple_of(pair * BLOCK, BLOCK), BLOCK)
        column = pl.multiple_of(own * COLS + pair * BLOCK, BLOCK)
        return remote(
            attended.at[step, lax.rem(c + dc, 2), :, lanes], out.at[0, :, pl.ds(column, BLOCK)],
            o_send.at[step, dc, pair], o_recv.at[step, dc, pair], target,
        )

    def out_own(pair):
        lanes = pl.ds(pl.multiple_of(pair * BLOCK, BLOCK), BLOCK)
        column = pl.multiple_of(own * COLS + pair * BLOCK, BLOCK)
        return pltpu.make_async_copy(
            attended.at[0, c, :, lanes], out.at[0, :, pl.ds(column, BLOCK)], o_local.at[pair]
        )

    def chip_of(step):
        away = jnp.where(step == 1, 3, jnp.where(step == 2, 1, jnp.where(step == 3, 2, 0)))
        return lax.rem(z + away, 4)

    first_head = lax.broadcasted_iota(jnp.int32, (2 * TOKENS, BLOCK), 1) < HDIM

    def one_chip(step, carry):
        chip = chip_of(step)

        @pl.when(step == 0)
        def _():
            patch_copy(6).wait_recv()

        @pl.when(step == 1)
        def _():
            patch_copy(1).wait_recv()
            patch_copy(7).start()
            patch_copy(3).wait_recv()
            patch_copy(8).start()
            patch_copy(7).wait_recv()

        @pl.when(step == 2)
        def _():
            patch_copy(8).wait_recv()
            patch_copy(4).wait_recv()
            patch_copy(5).wait_recv()
            patch_copy(9).start()

        @pl.when(step == 3)
        def _():
            patch_copy(9).wait_recv()

        rows = patch_all[pl.ds(chip * 2, 2)].reshape(2 * TOKENS, FEATURES)
        weight = weight_all[...].reshape(FEATURES, COLS)
        queries = jnp.dot(rows, weight, preferred_element_type=jnp.float32)
        for pair in range(PAIRS):
            block = queries[:, pair * BLOCK : (pair + 1) * BLOCK]
            gain = query_gain[:, pl.ds(pl.multiple_of(own * COLS + pair * BLOCK, BLOCK), BLOCK)]
            normed = pair_norm(block, split_dot(block, ones), gain, ones).astype(jnp.bfloat16)
            query_all[pair] = normed * jnp.bfloat16(0.125)

        def one_pair(pair, inner):
            @pl.when(step == 0)
            def _():
                for route in range(len(KV_ROUTES) + 1):
                    y_copy(pair, route).wait_recv()

            query = query_all[pair]
            key = kv_all[pair, 0].reshape(16 * TOKENS, BLOCK)
            value = kv_all[pair, 1].reshape(16 * TOKENS, BLOCK)
            halves = []
            for head in range(2):
                mine = first_head if head == 0 else jnp.logical_not(first_head)
                masked = jnp.where(mine, query, jnp.zeros_like(query))
                scores = lax.dot_general(
                    masked, key, (((1,), (1,)), ((), ())), preferred_element_type=jnp.float32
                )
                largest = jnp.max(scores, axis=1, keepdims=True)
                probability = jnp.exp(scores - largest)
                normaliser = jnp.sum(probability, axis=1, keepdims=True)
                blended = jnp.dot(
                    probability.astype(jnp.bfloat16), value, preferred_element_type=jnp.float32
                )
                halves.append(blended / normaliser)
            mixed = jnp.where(first_head, halves[0], halves[1]).astype(jnp.bfloat16)
            lanes = pl.ds(pl.multiple_of(pair * BLOCK, BLOCK), BLOCK)
            attended[step, :, :, lanes] = mixed.reshape(2, TOKENS, BLOCK)
            out_copy(step, chip, pair, 1).start()

            @pl.when(step == 0)
            def _():
                out_own(pair).start()

            @pl.when(step > 0)
            def _():
                out_copy(step, chip, pair, 0).start()

            return inner

        lax.fori_loop(0, PAIRS, one_pair, 0)
        return carry

    lax.fori_loop(0, 4, one_chip, 0)

    for copy in weight_y + weight_x + weight_x2:
        copy.wait_send()
    for pair in range(PAIRS):
        for route in range(len(KV_ROUTES)):
            kv_copy(pair, route).wait_send()
        for route in range(len(KV_ROUTES) + 1):
            y_copy(pair, route).wait_send()
    for which in range(10):
        patch_copy(which).wait_send()

    def finish(step, carry):
        chip = chip_of(step)
        for pair in range(PAIRS):
            out_copy(step, chip, pair, 1).wait()

            @pl.when(step == 0)
            def _():
                out_own(pair).wait()

            @pl.when(step > 0)
            def _():
                out_copy(step, chip, pair, 0).wait()

        return carry

    lax.fori_loop(0, 4, finish, 0)


def per_device(patches, weight_codes, block_scales, key_proj, value_proj, query_gain, key_gain):
    bf16 = jnp.bfloat16
    dma = pltpu.SemaphoreType.DMA
    anywhere = pl.BlockSpec(memory_space=pl.ANY)
    in_vmem = pl.BlockSpec(memory_space=pltpu.VMEM)
    return pl.pallas_call(
        kernel,
        out_shape=jax.ShapeDtypeStruct((1, TOKENS, FEATURES), bf16),
        in_specs=[
            anywhere, anywhere, pl.BlockSpec(memory_space=pltpu.SMEM), anywhere, anywhere, in_vmem, in_vmem,
        ],
        out_specs=anywhere,
        scratch_shapes=[
            pltpu.VMEM((8, TOKENS, FEATURES), bf16),
            pltpu.VMEM((8, ROWS, COLS), bf16),
            pltpu.VMEM((2, TOKENS, FEATURES), bf16),
            pltpu.VMEM((PAIRS, 2, 2, 8, TOKENS, BLOCK), bf16),
            pltpu.VMEM((ROWS, COLS), jnp.int32),
            pltpu.VMEM((PAIRS, 2 * TOKENS, BLOCK), bf16),
            pltpu.VMEM((4, 2, TOKENS, COLS), bf16),
            dma((4,)), dma((8,)), dma((8,)), dma((PAIRS, 7)), dma((PAIRS, 7)), dma((PAIRS, 8)), dma((PAIRS, 8)),
            dma((10,)), dma((10,)), dma((4, 2, PAIRS)), dma((4, 2, PAIRS)), dma((PAIRS,)),
        ],
        compiler_params=pltpu.CompilerParams(
            collective_id=0, has_side_effects=True, vmem_limit_bytes=60 * 1024 * 1024
        ),
        name="project_attend",
    )(
        patches, weight_codes, block_scales, key_proj, value_proj,
        query_gain.reshape(1, FEATURES), key_gain.reshape(1, FEATURES),
    )


def solution(mesh):
    grid = Mesh(mesh.devices.reshape(4, 2, 2, 2, 4), AXES)
    seq, fsdp = ("z", "yh", "c"), ("yl", "x")
    placed = (
        P(fsdp, seq, None), P(fsdp, None), P(fsdp, None), P(fsdp, seq, None), P(fsdp, seq, None), P(), P(),
    )
    return jax.shard_map(
        per_device, mesh=grid, in_specs=placed, out_specs=P(fsdp, seq, None), check_vma=False
    )
```

time: 282 us -> 84 us (0.30)
  waiting for transfers between devices: 152 us -> 0 us
  Pallas kernels: 0 us -> 81.7 us
  blocking collectives: 39.5 us -> 0 us
  matrix products: 28 us -> 0 us
  starting transfers between devices: 18 us -> 0 us
  other arithmetic: 16.6 us -> 0 us
  between operations: 13.6 us -> 0.01 us
  local copies, waits for them, and re-layouts: 13.6 us -> 2.06 us
    reduce_scatter x1 -> x0, waiting for transfers between devices: 119 us -> none  [per_device(): lax.psum_scatter(jnp.dot(group_rows, local_weight, preferred_element_type...]
    pallas_call x0 -> x1, Pallas kernels: none -> 81.7 us  [per_device(): pl.pallas_call(kernel, out_shape=jax.ShapeDtypeStruct((1, TOKENS, FEATURE...]
    all_to_all x3 -> x0, blocking collectives: 39.5 us -> none  [the longest x2 21.8 us: exchange_in_order(): whole = lax.all_to_all(whole, axes[k], k, k, tiled=True)]
    all_to_all x3 -> x0, waiting for transfers between devices: 32.8 us -> none  [the longest x1 12.8 us: per_device(): lax.all_to_all(query_view, SEQ, split_axis=2, concat_axis=1, tiled=True)]
    dot_general x9 -> x0, matrix products: 28 us -> none  [the longest x4 13.2 us: attend_block(): jnp.einsum('iths,ishd->ithd', probability.astype(jnp.bfloat16), value_vie...]
    all_to_all x3 -> x0, starting transfers between devices: 18 us -> none  [the longest x1 9.47 us: per_device(): lax.all_to_all(key_norm, SEQ, split_axis=2, concat_axis=1, tiled=True)]
    reduce_sum x8 -> x0, other arithmetic: 13.7 us -> none  [the longest x4 9.85 us: attend_block(): running_sum = jnp.sum(probability, axis=-1)]
    unnamed x17 -> x1, local copies, waits for them, and re-layouts: 6.11 us -> 2.06 us
  transfers between devices with their start and end apart: 4 -> 0, of which waited for: 4 -> 0; matrix products, arithmetic and copies ran while one was open for 3% -> 0% of each run, Pallas kernels for 0% -> 0%
where the time goes in v1:
time: 84 us; the launch traced here: 83.8 us
  Pallas kernels  81.7 us (97%)
  local copies, waits for them, and re-layouts  2.06 us (2%)
    pallas_call x1, Pallas kernels, per_device(): pl.pallas_call(kernel, out_shape=jax.ShapeDtypeStruct((1, TOKENS, FEATURE...  81.7 us
    unnamed x1, local copies, waits for them, and re-layouts  2.06 us

profile of v1, /device:TPU:1, one launch (start us, length us, event | category | flops | bytes accessed | tf_op | source)
XLA Modules:
  0.0 83.8 jit_solution(13796628834762950792)
XLA Ops:
  0.0 81.7 %project_attend.1 = bf16[1,128,3072]{2,1,0:T(8,128)(2,1)} custom-call(bf16[1,128,3072]{2,1,0:T(8,128)(2,1)} %patches.1, s32[384,3072]{1,0:T(8,128)} %codes.1, f32[3,24]{1,0:T(4,128)} %scales.1, bf16[1,128,3072]{2,1,0:T(8,128)(2,1)} %keys.1, bf16[1,128,3072]{2,1,0:T(8,128)(2,1)} %values.1, f32[1,3072]{1,0:T(1,128)} %bitcast.2, f32[1,3072]{1,0:T(1,128)} %bitcast.3), custom_call_target="tpu_custom_call" | custom-call | tf_op jit(solution)/shard_map/project_attend/pallas_call | solution.py:326
  81.7 2.1 %copy.9 = bf16[1,128,3072]{2,1,0:T(8,128)(2,1)} copy(bf16[1,128,3072]{2,1,0:T(8,128)(2,1)} %project_attend.1) | data formatting | bytes 1572864

commit v2 on v1

v2 whole, which is shorter than its diff:
```python
import jax
import jax.numpy as jnp
from jax import lax
from jax.experimental import pallas as pl
from jax.experimental.pallas import tpu as pltpu
from jax.sharding import Mesh
from jax.sharding import PartitionSpec as P

HDIM = 64
BLOCK = 128
NORM_FLOOR = 0.25
AXES = ("z", "yh", "c", "yl", "x")
MESH = pl.DeviceIdType.MESH

TOKENS = 128
FEATURES = 3072
ROWS = 384
PAIRS = 3
COLS = PAIRS * BLOCK
HALF = TOKENS // 2
KEYS = 16 * TOKENS
PIECE = 256

KV_ROUTES = ((0, 1), (1, 0), (1, 1), (3, 0), (3, 1), (2, 0), (2, 1))


def split_dot(values, ones):
    high = values.astype(jnp.bfloat16)
    low = (values - high.astype(jnp.float32)).astype(jnp.bfloat16)
    return jnp.dot(high, ones, preferred_element_type=jnp.float32) + jnp.dot(
        low, ones, preferred_element_type=jnp.float32
    )


def head_ones():
    row = lax.broadcasted_iota(jnp.int32, (BLOCK, BLOCK), 0) // HDIM
    column = lax.broadcasted_iota(jnp.int32, (BLOCK, BLOCK), 1) // HDIM
    return jnp.where(row == column, 1.0, 0.0).astype(jnp.bfloat16)


def pair_norm(values, total, gain_row, ones):
    centred = values - total * (1.0 / HDIM)
    spread = split_dot(centred * centred, ones) * (1.0 / HDIM)
    return centred * lax.rsqrt(spread + NORM_FLOOR) * gain_row


def kernel(
    patches, codes, scales, keys, values, query_gain, key_gain, out,
    patch_all, weight_all, own_kv, kv_all, code_block, query_all, attended,
    value_rows, scores_a, scores_b, largest_a, largest_b, blended_a,
    local_sem, w_send, w_recv, kv_send, kv_recv, y_send, y_recv, p_send, p_recv, o_send, o_recv,
):
    z, yh, c = lax.axis_index("z"), lax.axis_index("yh"), lax.axis_index("c")
    yl, x = lax.axis_index("yl"), lax.axis_index("x")
    y = yh * 2 + yl

    def at(dz=0, dy=0, dx=0, dc=0):
        row = lax.rem(y + dy, 4)
        return (
            lax.rem(z + dz, 4), lax.div(row, 2), lax.rem(c + dc, 2), lax.rem(row, 2), lax.rem(x + dx, 4),
        )

    def remote(source, target, send, recv, device):
        return pltpu.make_async_remote_copy(
            src_ref=source, dst_ref=target, send_sem=send, recv_sem=recv, device_id=device, device_id_type=MESH,
        )

    own = z * 2 + c
    chunk = yl * 4 + x
    first_column = pl.multiple_of(own * COLS, BLOCK)

    barrier = pltpu.get_barrier_semaphore()
    partners = [at(dz=dz, dc=dc) for dz, dc in KV_ROUTES]
    partners += [at(dy=dy) for dy in (1, 2, 3)] + [at(dx=dx) for dx in (1, 3)]
    for partner in partners:
        pl.semaphore_signal(barrier, inc=1, device_id=partner, device_id_type=MESH)

    load_codes = pltpu.make_async_copy(codes.at[:, pl.ds(first_column, COLS)], code_block, local_sem.at[0])
    load_keys = pltpu.make_async_copy(keys.at[0], own_kv.at[0], local_sem.at[1])
    load_values = pltpu.make_async_copy(values.at[0], own_kv.at[1], local_sem.at[2])
    load_patches = [
        pltpu.make_async_copy(
            patches.at[0, pl.ds(half * HALF, HALF)], patch_all.at[z, c, half], local_sem.at[3 + half]
        )
        for half in range(2)
    ]
    for load in [load_values, load_codes, load_keys] + load_patches:
        load.start()

    load_codes.wait()
    for r in range(ROWS // BLOCK):
        for k in range(PAIRS):
            block = code_block[r * BLOCK : (r + 1) * BLOCK, k * BLOCK : (k + 1) * BLOCK]
            weight_all[chunk, r * BLOCK : (r + 1) * BLOCK, k * BLOCK : (k + 1) * BLOCK] = (
                block.astype(jnp.float32) * scales[r, own * PAIRS + k]
            ).astype(jnp.bfloat16)

    half_rows = ROWS // 2
    def weight_copy(which):
        low, high = (0, half_rows), (half_rows, half_rows)
        before, after = lax.rem(x + 3, 4), lax.rem(x + 1, 4)
        row, place, rows, target = (
            (yl, x, low, at(dy=1)), (yl, x, high, at(dy=3)),
            (yl, x, None, at(dx=1)), (yl, x, None, at(dx=3)),
            (1 - yl, x, None, at(dx=1)), (1 - yl, x, None, at(dx=3)),
            (yl, before, low, at(dx=1)), (yl, after, high, at(dx=3)),
            (1 - yl, before, low, at(dx=1)), (1 - yl, after, high, at(dx=3)),
        )[which]
        block = weight_all.at[row * 4 + place]
        if rows is not None:
            block = weight_all.at[row * 4 + place, pl.ds(*rows)]
        return remote(block, block, w_send.at[which], w_recv.at[which], target)

    routes = len(KV_ROUTES)

    def kv_copy(part, pair, route):
        dz, dc = KV_ROUTES[route]
        target = at(dz=dz, dc=dc)
        column = pl.multiple_of((target[0] * 2 + target[2]) * COLS + pair * BLOCK, BLOCK)
        return remote(
            own_kv.at[part, :, pl.ds(column, BLOCK)], kv_all.at[pair, part, yh, own],
            kv_send.at[part, pair, route], kv_recv.at[part, pair, route], target,
        )

    def slot_of(route):
        if route == routes:
            return own
        dz, dc = KV_ROUTES[route]
        return lax.rem(z + 4 - dz, 4) * 2 + lax.rem(c + dc, 2)

    def y_copy(part, pair, route):
        place = kv_all.at[pair, part, yh, slot_of(route)]
        return remote(place, place, y_send.at[part, pair, route], y_recv.at[part, pair, route], at(dy=2))

    def send_kv(part, pair):
        for route in range(routes):
            kv_copy(part, pair, route).start()
        column = pl.multiple_of(own * COLS + pair * BLOCK, BLOCK)
        kv_all[pair, part, yh, own] = own_kv[part, :, pl.ds(column, BLOCK)]

    def forward_kv(part, pair):
        y_copy(part, pair, routes).start()
        for route in range(routes):
            kv_copy(part, pair, route).wait_recv()
            y_copy(part, pair, route).start()

    down, up, across = lax.rem(z + 3, 4), lax.rem(z + 1, 4), lax.rem(z + 2, 4)

    def patch_copy(which):
        place, target = (
            ((z, c, 0), at(dz=1)), ((z, c, 1), at(dz=3)), ((z, c, 1), at(dz=1)), ((z, c, 0), at(dz=3)),
            ((down, c, 0), at(dz=1)), ((up, c, 1), at(dz=3)),
            ((z, c), at(dc=1)), ((down, c, 0), at(dc=1)), ((up, c, 1), at(dc=1)),
            ((down, c, 1), at(dc=1)), ((up, c, 0), at(dc=1)),
            ((across, c, 0), at(dc=1)), ((across, c, 1), at(dc=1)),
        )[which]
        block = patch_all.at[place]
        return remote(block, block, p_send.at[which], p_recv.at[which], target)

    ones = head_ones()

    def normalize_keys(pair):
        for owner in range(8):
            lanes = slice((owner * PAIRS + pair) * BLOCK, (owner * PAIRS + pair + 1) * BLOCK)
            block = own_kv[0, :, lanes]
            total = jnp.dot(block, ones, preferred_element_type=jnp.float32)
            own_kv[0, :, lanes] = pair_norm(
                block.astype(jnp.float32), total, key_gain[:, lanes], ones
            ).astype(jnp.bfloat16)

    def forward_weight(first):
        for which in (first, first + 1):
            weight_copy(which).wait_recv()
            weight_copy(which + 4).start()

    load_keys.wait()
    normalize_keys(0)
    load_values.wait()
    for load in load_patches:
        load.wait()
    pl.semaphore_wait(barrier, len(partners))
    for which in range(4):
        weight_copy(which).start()
    patch_copy(6).start()
    send_kv(1, 0)
    send_kv(0, 0)
    normalize_keys(1)
    send_kv(1, 1)
    send_kv(0, 1)
    for which in (0, 1):
        patch_copy(which).start()
    normalize_keys(2)
    send_kv(1, 2)
    send_kv(0, 2)
    for which in (2, 3):
        patch_copy(which).start()
    for which in range(2):
        weight_copy(which).wait_recv()
    for which in range(4, 6):
        weight_copy(which).start()
    forward_kv(1, 0)
    forward_kv(0, 0)
    forward_weight(2)
    forward_kv(1, 1)
    forward_kv(0, 1)
    forward_weight(4)
    for which in range(6, 10):
        weight_copy(which).wait_recv()

    def piece_of(group, k):
        beside = down if k == 0 else up
        chip = jnp.where(group == 0, z, jnp.where(group == 3, across, beside))
        half = jnp.where(group == 2, 1 - k, k)
        return chip, half

    def out_copy(group, pair, dc, k):
        chip, half = piece_of(group, k)
        target = (chip, yh, lax.rem(c + dc, 2), yl, x)
        lanes = pl.ds(pl.multiple_of(pair * BLOCK, BLOCK), BLOCK)
        column = pl.multiple_of(own * COLS + pair * BLOCK, BLOCK)
        rows = pl.ds(pl.multiple_of(half * HALF, HALF), HALF)
        return remote(
            attended.at[group, dc, k, :, lanes], out.at[0, rows, pl.ds(column, BLOCK)],
            o_send.at[group, pair, dc, k], o_recv.at[group, pair, dc, k], target,
        )

    def out_own(pair, k):
        lanes = pl.ds(pl.multiple_of(pair * BLOCK, BLOCK), BLOCK)
        column = pl.multiple_of(own * COLS + pair * BLOCK, BLOCK)
        return pltpu.make_async_copy(
            attended.at[0, 0, k, :, lanes], out.at[0, pl.ds(k * HALF, HALF), pl.ds(column, BLOCK)],
            o_send.at[0, pair, 0, k],
        )

    first_head = lax.broadcasted_iota(jnp.int32, (2 * TOKENS, BLOCK), 1) < HDIM

    def project(group):
        pieces = []
        for dc in range(2):
            for k in range(2):
                chip, half = piece_of(group, k)
                pieces.append(patch_all[chip, lax.rem(c + dc, 2), half])
        rows = jnp.concatenate(pieces, axis=0)
        weight = weight_all[...].reshape(FEATURES, COLS)
        queries = jnp.dot(rows, weight, preferred_element_type=jnp.float32)
        for pair in range(PAIRS):
            block = queries[:, pair * BLOCK : (pair + 1) * BLOCK]
            gain = query_gain[:, pl.ds(pl.multiple_of(own * COLS + pair * BLOCK, BLOCK), BLOCK)]
            normed = pair_norm(block, split_dot(block, ones), gain, ones).astype(jnp.bfloat16)
            normed = normed * jnp.bfloat16(0.125)
            query_all[group, pair, 0] = jnp.where(first_head, normed, jnp.zeros_like(normed))
            query_all[group, pair, 1] = jnp.where(first_head, jnp.zeros_like(normed), normed)

    def group_of(task):
        return jnp.where(task < 4, lax.rem(task, 2), jnp.where(task < 6, 2, jnp.where(task < 9, task - 6, 3)))

    def pair_of(task):
        return jnp.where(task < 4, lax.div(task, 2), jnp.where(task < 6, task - 4, jnp.where(task < 9, 2, task - 9)))

    def any_of(task, *which):
        found = task == which[0]
        for other in which[1:]:
            found = jnp.logical_or(found, task == other)
        return found

    def prepare(task):
        @pl.when(task == 0)
        def _():
            patch_copy(6).wait_recv()

        @pl.when(task == 1)
        def _():
            for which in (0, 1):
                patch_copy(which).wait_recv()
                patch_copy(which + 4).start()
                patch_copy(which + 7).start()
            for which in (7, 8):
                patch_copy(which).wait_recv()

        @pl.when(task == 2)
        def _():
            forward_kv(1, 2)

        @pl.when(task == 3)
        def _():
            forward_kv(0, 2)

        @pl.when(task == 4)
        def _():
            for which in (2, 3):
                patch_copy(which).wait_recv()
                patch_copy(which + 7).start()
            for which in (9, 10):
                patch_copy(which).wait_recv()

        @pl.when(task == 8)
        def _():
            for which in (4, 5):
                patch_copy(which).wait_recv()
                patch_copy(which + 7).start()

        @pl.when(task == 9)
        def _():
            for which in (11, 12):
                patch_copy(which).wait_recv()

        @pl.when(any_of(task, 0, 1, 4, 9))
        def _():
            project(group_of(task))

        @pl.when(any_of(task, 0, 2, 6))
        def _():
            pair = pair_of(task)
            for part in (1, 0):
                for route in range(routes + 1):
                    y_copy(part, pair, route).wait_recv()
            value_rows[pair] = kv_all[pair, 1].reshape(KEYS, BLOCK).T

    def score_piece(task, head, piece, held):
        key = kv_all[pair_of(task), 0, piece // 4, piece % 4 * 2 : piece % 4 * 2 + 2].reshape(PIECE, BLOCK)
        scores = lax.dot_general(
            key, query_all[group_of(task), pair_of(task), head], (((1,), (1,)), ((), ())),
            preferred_element_type=jnp.float32,
        )
        held[piece * PIECE : (piece + 1) * PIECE] = scores
        return jnp.max(scores, axis=0, keepdims=True)

    def blend_piece(task, head, piece, held, largest):
        probability = jnp.exp(held[piece * PIECE : (piece + 1) * PIECE] - largest)
        value = value_rows[
            pair_of(task), head * HDIM : (head + 1) * HDIM, piece * PIECE : (piece + 1) * PIECE
        ]
        return jnp.dot(
            value, probability.astype(jnp.bfloat16), preferred_element_type=jnp.float32
        ), jnp.sum(probability, axis=0, keepdims=True)

    def stage(done_task, done_head, held, largest_ref, next_task, next_head, next_held, next_largest_ref):
        largest = largest_ref[...]
        best = blended = total = None
        for piece in range(KEYS // PIECE):
            tops = score_piece(next_task, next_head, piece, next_held)
            product, part = blend_piece(done_task, done_head, piece, held, largest)
            best = tops if piece == 0 else jnp.maximum(best, tops)
            blended = product if piece == 0 else blended + product
            total = part if piece == 0 else total + part
        next_largest_ref[...] = best
        return blended / total

    prepare(0)
    best = None
    for piece in range(KEYS // PIECE):
        tops = score_piece(0, 0, piece, scores_a)
        best = tops if piece == 0 else jnp.maximum(best, tops)
    largest_a[...] = best

    def one_task(task, carry):
        following = jnp.minimum(task + 1, 4 * PAIRS - 1)
        blended_a[...] = stage(task, 0, scores_a, largest_a, task, 1, scores_b, largest_b)

        @pl.when(task < 4 * PAIRS - 1)
        def _():
            prepare(task + 1)

        second = stage(task, 1, scores_b, largest_b, following, 0, scores_a, largest_a)
        mixed = jnp.concatenate([blended_a[...], second], axis=0).T.astype(jnp.bfloat16)
        group, pair = group_of(task), pair_of(task)
        lanes = pl.ds(pl.multiple_of(pair * BLOCK, BLOCK), BLOCK)
        attended[group, :, :, :, lanes] = mixed.reshape(2, 2, HALF, BLOCK)
        @pl.when(group == 0)
        def _():
            for k in range(2):
                out_copy(group, pair, 1, k).start()
                out_own(pair, k).start()

        @pl.when(task == 7)
        def _():
            for held_group, held_pair in ((1, 0), (1, 1), (2, 0), (2, 1), (1, 2)):
                for dc in range(2):
                    for k in range(2):
                        out_copy(held_group, held_pair, dc, k).start()

        @pl.when(task >= 8)
        def _():
            for dc in range(2):
                for k in range(2):
                    out_copy(group, pair, dc, k).start()

        return carry

    lax.fori_loop(0, 4 * PAIRS, one_task, 0)

    for which in range(10):
        weight_copy(which).wait_send()
    for part in range(2):
        for pair in range(PAIRS):
            for route in range(routes):
                kv_copy(part, pair, route).wait_send()
            for route in range(routes + 1):
                y_copy(part, pair, route).wait_send()
    for which in range(13):
        patch_copy(which).wait_send()

    def finish(group, carry):
        for pair in range(PAIRS):
            for k in range(2):
                out_copy(group, pair, 1, k).wait()

                @pl.when(group == 0)
                def _():
                    out_own(pair, k).wait()

                @pl.when(group > 0)
                def _():
                    out_copy(group, pair, 0, k).wait()

        return carry

    lax.fori_loop(0, 4, finish, 0)


def per_device(patches, weight_codes, block_scales, key_proj, value_proj, query_gain, key_gain):
    bf16, f32 = jnp.bfloat16, jnp.float32
    dma = pltpu.SemaphoreType.DMA
    anywhere = pl.BlockSpec(memory_space=pl.ANY)
    in_vmem = pl.BlockSpec(memory_space=pltpu.VMEM)
    return pl.pallas_call(
        kernel,
        out_shape=jax.ShapeDtypeStruct((1, TOKENS, FEATURES), bf16),
        in_specs=[
            anywhere, anywhere, pl.BlockSpec(memory_space=pltpu.SMEM), anywhere, anywhere, in_vmem, in_vmem,
        ],
        out_specs=anywhere,
        scratch_shapes=[
            pltpu.VMEM((4, 2, 2, HALF, FEATURES), bf16),
            pltpu.VMEM((8, ROWS, COLS), bf16),
            pltpu.VMEM((2, TOKENS, FEATURES), bf16),
            pltpu.VMEM((PAIRS, 2, 2, 8, TOKENS, BLOCK), bf16),
            pltpu.VMEM((ROWS, COLS), jnp.int32),
            pltpu.VMEM((4, PAIRS, 2, 2 * TOKENS, BLOCK), bf16),
            pltpu.VMEM((4, 2, 2, HALF, COLS), bf16),
            pltpu.VMEM((PAIRS, BLOCK, KEYS), bf16),
            pltpu.VMEM((KEYS, 2 * TOKENS), f32),
            pltpu.VMEM((KEYS, 2 * TOKENS), f32),
            pltpu.VMEM((1, 2 * TOKENS), f32),
            pltpu.VMEM((1, 2 * TOKENS), f32),
            pltpu.VMEM((HDIM, 2 * TOKENS), f32),
            dma((5,)), dma((10,)), dma((10,)), dma((2, PAIRS, 7)), dma((2, PAIRS, 7)), dma((2, PAIRS, 8)),
            dma((2, PAIRS, 8)), dma((13,)), dma((13,)), dma((4, PAIRS, 2, 2)), dma((4, PAIRS, 2, 2)),
        ],
        compiler_params=pltpu.CompilerParams(
            collective_id=0, has_side_effects=True, vmem_limit_bytes=60 * 1024 * 1024
        ),
        name="project_attend",
    )(
        patches, weight_codes, block_scales, key_proj, value_proj,
        query_gain.reshape(1, FEATURES), key_gain.reshape(1, FEATURES),
    )


def solution(mesh):
    grid = Mesh(mesh.devices.reshape(4, 2, 2, 2, 4), AXES)
    seq, fsdp = ("z", "yh", "c"), ("yl", "x")
    placed = (
        P(fsdp, seq, None), P(fsdp, None), P(fsdp, None), P(fsdp, seq, None), P(fsdp, seq, None), P(), P(),
    )
    return jax.shard_map(
        per_device, mesh=grid, in_specs=placed, out_specs=P(fsdp, seq, None), check_vma=False
    )
```

time: 84 us -> 72.9 us (0.87)
  Pallas kernels: 81.7 us -> 70.6 us
    pallas_call x1, Pallas kernels: 81.7 us -> 70.6 us  [per_device(): pl.pallas_call(kernel, out_shape=jax.ShapeDtypeStruct((1, TOKENS, FEATURE...]
where the time goes in v2:
time: 72.9 us; the launch traced here: 72.6 us
  Pallas kernels  70.6 us (97%)
  local copies, waits for them, and re-layouts  2.06 us (3%)
    pallas_call x1, Pallas kernels, per_device(): pl.pallas_call(kernel, out_shape=jax.ShapeDtypeStruct((1, TOKENS, FEATURE...  70.6 us
    unnamed x1, local copies, waits for them, and re-layouts  2.06 us

profile of v2, /device:TPU:1, one launch (start us, length us, event | category | flops | bytes accessed | tf_op | source)
XLA Modules:
  0.0 72.6 jit_solution(4126304732573473676)
XLA Ops:
  0.0 70.6 %project_attend.1 = bf16[1,128,3072]{2,1,0:T(8,128)(2,1)} custom-call(bf16[1,128,3072]{2,1,0:T(8,128)(2,1)} %patches.1, s32[384,3072]{1,0:T(8,128)} %codes.1, f32[3,24]{1,0:T(4,128)} %scales.1, bf16[1,128,3072]{2,1,0:T(8,128)(2,1)} %keys.1, bf16[1,128,3072]{2,1,0:T(8,128)(2,1)} %values.1, f32[1,3072]{1,0:T(1,128)} %bitcast.2, f32[1,3072]{1,0:T(1,128)} %bitcast.3), custom_call_target="tpu_custom_call" | custom-call | tf_op jit(solution)/shard_map/project_attend/pallas_call | solution.py:426
  70.6 2.1 %copy.9 = bf16[1,128,3072]{2,1,0:T(8,128)(2,1)} copy(bf16[1,128,3072]{2,1,0:T(8,128)(2,1)} %project_attend.1) | data formatting | bytes 1572864

commit v3 on v2

--- a/solution.py
+++ b/solution.py
@@ -137,9 +137,12 @@
             kv_copy(part, pair, route).start()
         column = pl.multiple_of(own * COLS + pair * BLOCK, BLOCK)
         kv_all[pair, part, yh, own] = own_kv[part, :, pl.ds(column, BLOCK)]
+        if pair < 2:
+            y_copy(part, pair, routes).start()
 
     def forward_kv(part, pair):
-        y_copy(part, pair, routes).start()
+        if pair == 2:
+            y_copy(part, pair, routes).start()
         for route in range(routes):
             kv_copy(part, pair, route).wait_recv()
             y_copy(part, pair, route).start()
@@ -251,18 +254,20 @@
             query_all[group, pair, 0] = jnp.where(first_head, normed, jnp.zeros_like(normed))
             query_all[group, pair, 1] = jnp.where(first_head, jnp.zeros_like(normed), normed)
 
-    def group_of(task):
-        return jnp.where(task < 4, lax.rem(task, 2), jnp.where(task < 6, 2, jnp.where(task < 9, task - 6, 3)))
-
-    def pair_of(task):
-        return jnp.where(task < 4, lax.div(task, 2), jnp.where(task < 6, task - 4, jnp.where(task < 9, 2, task - 9)))
-
     def any_of(task, *which):
         found = task == which[0]
         for other in which[1:]:
             found = jnp.logical_or(found, task == other)
         return found
 
+    def group_of(task):
+        late = jnp.where(task == 6, 2, jnp.where(task == 7, 1, jnp.where(task == 11, 0, 3)))
+        return jnp.where(task < 4, lax.rem(task, 2), jnp.where(task < 6, 2, late))
+
+    def pair_of(task):
+        late = jnp.where(any_of(task, 8, 9), task - 8, 2)
+        return jnp.where(task < 4, lax.div(task, 2), jnp.where(task < 6, task - 4, late))
+
     def prepare(task):
         @pl.when(task == 0)
         def _():
@@ -276,12 +281,9 @@
                 patch_copy(which + 7).start()
             for which in (7, 8):
                 patch_copy(which).wait_recv()
+            forward_kv(1, 2)
 
         @pl.when(task == 2)
-        def _():
-            forward_kv(1, 2)
-
-        @pl.when(task == 3)
         def _():
             forward_kv(0, 2)
 
@@ -295,16 +297,10 @@
 
         @pl.when(task == 8)
         def _():
-            for which in (4, 5):
-                patch_copy(which).wait_recv()
-                patch_copy(which + 7).start()
-
-        @pl.when(task == 9)
-        def _():
             for which in (11, 12):
                 patch_copy(which).wait_recv()
 
-        @pl.when(any_of(task, 0, 1, 4, 9))
+        @pl.when(any_of(task, 0, 1, 4, 8))
         def _():
             project(group_of(task))
 
@@ -355,6 +351,13 @@
 
     def one_task(task, carry):
         following = jnp.minimum(task + 1, 4 * PAIRS - 1)
+
+        @pl.when(task == 7)
+        def _():
+            for which in (4, 5):
+                patch_copy(which).wait_recv()
+                patch_copy(which + 7).start()
+
         blended_a[...] = stage(task, 0, scores_a, largest_a, task, 1, scores_b, largest_b)
 
         @pl.when(task < 4 * PAIRS - 1)
@@ -372,14 +375,7 @@
                 out_copy(group, pair, 1, k).start()
                 out_own(pair, k).start()
 
-        @pl.when(task == 7)
-        def _():
-            for held_group, held_pair in ((1, 0), (1, 1), (2, 0), (2, 1), (1, 2)):
-                for dc in range(2):
-                    for k in range(2):
-                        out_copy(held_group, held_pair, dc, k).start()
-
-        @pl.when(task >= 8)
+        @pl.when(group > 0)
         def _():
             for dc in range(2):
                 for k in range(2):
@@ -423,7 +419,7 @@
     dma = pltpu.SemaphoreType.DMA
     anywhere = pl.BlockSpec(memory_space=pl.ANY)
     in_vmem = pl.BlockSpec(memory_space=pltpu.VMEM)
-    return pl.pallas_call(
+    mixed = pl.pallas_call(
         kernel,
         out_shape=jax.ShapeDtypeStruct((1, TOKENS, FEATURES), bf16),
         in_specs=[
@@ -455,6 +451,16 @@
         patches, weight_codes, block_scales, key_proj, value_proj,
         query_gain.reshape(1, FEATURES), key_gain.reshape(1, FEATURES),
     )
+    def place(source, target):
+        target[...] = source[...]
+    return pl.pallas_call(
+        place,
+        out_shape=jax.ShapeDtypeStruct((1, TOKENS, FEATURES), bf16),
+        grid=(2,),
+        in_specs=[pl.BlockSpec((1, TOKENS // 2, FEATURES), lambda i: (0, i, 0))],
+        out_specs=pl.BlockSpec((1, TOKENS // 2, FEATURES), lambda i: (0, i, 0)),
+        name="place",
+    )(mixed)
 
 
 def solution(mesh):

time: 72.9 us -> 70.8 us (0.971)
  local copies, waits for them, and re-layouts: 2.06 us -> 0 us
    unnamed x1 -> x0, local copies, waits for them, and re-layouts: 2.06 us -> none
    pallas_call x0 -> x1, Pallas kernels: none -> 1.91 us  [per_device(): pl.pallas_call(place, out_shape=jax.ShapeDtypeStruct((1, TOKENS, FEATURES...]
    pallas_call x1, Pallas kernels: 70.6 us -> 68.7 us  [per_device(): pl.pallas_call(kernel, out_shape=jax.ShapeDtypeStruct((1, TOKENS, FEATURE...]
where the time goes in v3:
time: 70.8 us; the launch traced here: 70.6 us
  Pallas kernels  70.6 us (100%)
    pallas_call x1, Pallas kernels, per_device(): pl.pallas_call(kernel, out_shape=jax.ShapeDtypeStruct((1, TOKENS, FEATURE...  68.7 us
    pallas_call x1, Pallas kernels, per_device(): pl.pallas_call(place, out_shape=jax.ShapeDtypeStruct((1, TOKENS, FEATURES...  1.91 us

profile of v3, /device:TPU:1, one launch (start us, length us, event | category | flops | bytes accessed | tf_op | source)
XLA Modules:
  0.0 70.6 jit_solution(16790867218737697028)
XLA Ops:
  0.0 68.7 %project_attend.1.source = bf16[1,128,3072]{2,1,0:T(8,128)(2,1)} custom-call(bf16[1,128,3072]{2,1,0:T(8,128)(2,1)} %patches.1, s32[384,3072]{1,0:T(8,128)} %codes.1, f32[3,24]{1,0:T(4,128)} %scales.1, bf16[1,128,3072]{2,1,0:T(8,128)(2,1)} %keys.1, bf16[1,128,3072]{2,1,0:T(8,128)(2,1)} %values.1, f32[1,3072]{1,0:T(1,128)} %bitcast.2, f32[1,3072]{1,0:T(1,128)} %bitcast.3), custom_call_target="tpu_custom_call" | custom-call | tf_op jit(solution)/shard_map/project_attend/pallas_call | solution.py:422
  68.7 1.9 %place.1 = bf16[1,128,3072]{2,1,0:T(8,128)(2,1)} custom-call(bf16[1,128,3072]{2,1,0:T(8,128)(2,1)} %project_attend.1.source), custom_call_target="tpu_custom_call" | custom-call | tf_op jit(solution)/shard_map/place/pallas_call | solution.py:456

commit v4 on v3

--- a/solution.py
+++ b/solution.py
@@ -20,6 +20,7 @@
 HALF = TOKENS // 2
 KEYS = 16 * TOKENS
 PIECE = 256
+PART = FEATURES // 2
 
 KV_ROUTES = ((0, 1), (1, 0), (1, 1), (3, 0), (3, 1), (2, 0), (2, 1))
 
@@ -27,8 +28,9 @@
 def split_dot(values, ones):
     high = values.astype(jnp.bfloat16)
     low = (values - high.astype(jnp.float32)).astype(jnp.bfloat16)
-    return jnp.dot(high, ones, preferred_element_type=jnp.float32) + jnp.dot(
-        low, ones, preferred_element_type=jnp.float32
+    return jnp.dot(
+        jnp.concatenate([high, low], axis=1), jnp.concatenate([ones, ones], axis=0),
+        preferred_element_type=jnp.float32,
     )
 
 
@@ -47,7 +49,7 @@
 def kernel(
     patches, codes, scales, keys, values, query_gain, key_gain, out,
     patch_all, weight_all, own_kv, kv_all, code_block, query_all, attended,
-    value_rows, scores_a, scores_b, largest_a, largest_b, blended_a,
+    value_rows, scores_a, scores_b, largest_a, largest_b, blended_a, partial,
     local_sem, w_send, w_recv, kv_send, kv_recv, y_send, y_recv, p_send, p_recv, o_send, o_recv,
 ):
     z, yh, c = lax.axis_index("z"), lax.axis_index("yh"), lax.axis_index("c")
@@ -149,16 +151,16 @@
 
     down, up, across = lax.rem(z + 3, 4), lax.rem(z + 1, 4), lax.rem(z + 2, 4)
 
-    def patch_copy(which):
+    def patch_copy(which, part):
         place, target = (
             ((z, c, 0), at(dz=1)), ((z, c, 1), at(dz=3)), ((z, c, 1), at(dz=1)), ((z, c, 0), at(dz=3)),
             ((down, c, 0), at(dz=1)), ((up, c, 1), at(dz=3)),
-            ((z, c), at(dc=1)), ((down, c, 0), at(dc=1)), ((up, c, 1), at(dc=1)),
+            ((z, c, slice(None)), at(dc=1)), ((down, c, 0), at(dc=1)), ((up, c, 1), at(dc=1)),
             ((down, c, 1), at(dc=1)), ((up, c, 0), at(dc=1)),
             ((across, c, 0), at(dc=1)), ((across, c, 1), at(dc=1)),
         )[which]
-        block = patch_all.at[place]
-        return remote(block, block, p_send.at[which], p_recv.at[which], target)
+        block = patch_all.at[(*place, slice(None), pl.ds(part * PART, PART))]
+        return remote(block, block, p_send.at[which, part], p_recv.at[which, part], target)
 
     ones = head_ones()
 
@@ -184,19 +186,22 @@
     pl.semaphore_wait(barrier, len(partners))
     for which in range(4):
         weight_copy(which).start()
-    patch_copy(6).start()
+    for part in range(2):
+        patch_copy(6, part).start()
     send_kv(1, 0)
     send_kv(0, 0)
     normalize_keys(1)
     send_kv(1, 1)
     send_kv(0, 1)
-    for which in (0, 1):
-        patch_copy(which).start()
+    for part in range(2):
+        for which in (0, 1):
+            patch_copy(which, part).start()
     normalize_keys(2)
     send_kv(1, 2)
     send_kv(0, 2)
-    for which in (2, 3):
-        patch_copy(which).start()
+    for part in range(2):
+        for which in (2, 3):
+            patch_copy(which, part).start()
     for which in range(2):
         weight_copy(which).wait_recv()
     for which in range(4, 6):
@@ -237,15 +242,17 @@
 
     first_head = lax.broadcasted_iota(jnp.int32, (2 * TOKENS, BLOCK), 1) < HDIM
 
-    def project(group):
+    def project(group, part):
         pieces = []
         for dc in range(2):
             for k in range(2):
                 chip, half = piece_of(group, k)
-                pieces.append(patch_all[chip, lax.rem(c + dc, 2), half])
+                pieces.append(patch_all[chip, lax.rem(c + dc, 2), half, :, part * PART : (part + 1) * PART])
         rows = jnp.concatenate(pieces, axis=0)
-        weight = weight_all[...].reshape(FEATURES, COLS)
-        queries = jnp.dot(rows, weight, preferred_element_type=jnp.float32)
+        weight = weight_all[part * 4 : (part + 1) * 4].reshape(PART, COLS)
+        return jnp.dot(rows, weight, preferred_element_type=jnp.float32)
+
+    def normalize_queries(group, queries):
         for pair in range(PAIRS):
             block = queries[:, pair * BLOCK : (pair + 1) * BLOCK]
             gain = query_gain[:, pl.ds(pl.multiple_of(own * COLS + pair * BLOCK, BLOCK), BLOCK)]
@@ -269,40 +276,62 @@
         return jnp.where(task < 4, lax.div(task, 2), jnp.where(task < 6, task - 4, late))
 
     def prepare(task):
+        def arrive(*which):
+            for part in range(2):
+                for other in which:
+                    patch_copy(other, part).wait_recv()
+
         @pl.when(task == 0)
         def _():
-            patch_copy(6).wait_recv()
+            arrive(6)
 
         @pl.when(task == 1)
         def _():
-            for which in (0, 1):
-                patch_copy(which).wait_recv()
-                patch_copy(which + 4).start()
-                patch_copy(which + 7).start()
-            for which in (7, 8):
-                patch_copy(which).wait_recv()
+            for part in range(2):
+                for which in (0, 1):
+                    patch_copy(which, part).wait_recv()
+                    patch_copy(which + 4, part).start()
+                    patch_copy(which + 7, part).start()
+            arrive(7, 8)
             forward_kv(1, 2)
 
         @pl.when(task == 2)
         def _():
             forward_kv(0, 2)
 
-        @pl.when(task == 4)
-        def _():
-            for which in (2, 3):
-                patch_copy(which).wait_recv()
-                patch_copy(which + 7).start()
-            for which in (9, 10):
-                patch_copy(which).wait_recv()
-
-        @pl.when(task == 8)
-        def _():
-            for which in (11, 12):
-                patch_copy(which).wait_recv()
-
         @pl.when(any_of(task, 0, 1, 4, 8))
         def _():
-            project(group_of(task))
+            group = group_of(task)
+
+            @pl.when(task == 4)
+            def _():
+                for which in (2, 3):
+                    patch_copy(which, 0).wait_recv()
+                    patch_copy(which + 7, 0).start()
+                for which in (9, 10):
+                    patch_copy(which, 0).wait_recv()
+
+            @pl.when(task == 8)
+            def _():
+                for which in (11, 12):
+                    patch_copy(which, 0).wait_recv()
+
+            partial[...] = project(group, 0)
+
+            @pl.when(task == 4)
+            def _():
+                for which in (2, 3):
+                    patch_copy(which, 1).wait_recv()
+                    patch_copy(which + 7, 1).start()
+                for which in (9, 10):
+                    patch_copy(which, 1).wait_recv()
+
+            @pl.when(task == 8)
+            def _():
+                for which in (11, 12):
+                    patch_copy(which, 1).wait_recv()
+
+            normalize_queries(group, partial[...] + project(group, 1))
 
         @pl.when(any_of(task, 0, 2, 6))
         def _():
@@ -352,11 +381,13 @@
     def one_task(task, carry):
         following = jnp.minimum(task + 1, 4 * PAIRS - 1)
 
-        @pl.when(task == 7)
-        def _():
-            for which in (4, 5):
-                patch_copy(which).wait_recv()
-                patch_copy(which + 7).start()
+        for at_task, part in ((6, 0), (7, 1)):
+
+            @pl.when(task == at_task)
+            def _():
+                for which in (4, 5):
+                    patch_copy(which, part).wait_recv()
+                    patch_copy(which + 7, part).start()
 
         blended_a[...] = stage(task, 0, scores_a, largest_a, task, 1, scores_b, largest_b)
 
@@ -365,7 +396,7 @@
             prepare(task + 1)
 
         second = stage(task, 1, scores_b, largest_b, following, 0, scores_a, largest_a)
-        mixed = jnp.concatenate([blended_a[...], second], axis=0).T.astype(jnp.bfloat16)
+        mixed = jnp.concatenate([blended_a[...], second], axis=0).astype(jnp.bfloat16).T
         group, pair = group_of(task), pair_of(task)
         lanes = pl.ds(pl.multiple_of(pair * BLOCK, BLOCK), BLOCK)
         attended[group, :, :, :, lanes] = mixed.reshape(2, 2, HALF, BLOCK)
@@ -394,7 +425,8 @@
             for route in range(routes + 1):
                 y_copy(part, pair, route).wait_send()
     for which in range(13):
-        patch_copy(which).wait_send()
+        for part in range(2):
+            patch_copy(which, part).wait_send()
 
     def finish(group, carry):
         for pair in range(PAIRS):
@@ -440,8 +472,9 @@
             pltpu.VMEM((1, 2 * TOKENS), f32),
             pltpu.VMEM((1, 2 * TOKENS), f32),
             pltpu.VMEM((HDIM, 2 * TOKENS), f32),
+            pltpu.VMEM((2 * TOKENS, COLS), f32),
             dma((5,)), dma((10,)), dma((10,)), dma((2, PAIRS, 7)), dma((2, PAIRS, 7)), dma((2, PAIRS, 8)),
-            dma((2, PAIRS, 8)), dma((13,)), dma((13,)), dma((4, PAIRS, 2, 2)), dma((4, PAIRS, 2, 2)),
+            dma((2, PAIRS, 8)), dma((13, 2)), dma((13, 2)), dma((4, PAIRS, 2, 2)), dma((4, PAIRS, 2, 2)),
         ],
         compiler_params=pltpu.CompilerParams(
             collective_id=0, has_side_effects=True, vmem_limit_bytes=60 * 1024 * 1024

time: 70.8 us -> 69.6 us (0.983)
  Pallas kernels: 70.6 us -> 69.4 us
    pallas_call x1, Pallas kernels: 68.7 us -> 67.5 us  [per_device(): pl.pallas_call(kernel, out_shape=jax.ShapeDtypeStruct((1, TOKENS, FEATURE...]
where the time goes in v4:
time: 69.6 us; the launch traced here: 69.4 us
  Pallas kernels  69.4 us (100%)
    pallas_call x1, Pallas kernels, per_device(): pl.pallas_call(kernel, out_shape=jax.ShapeDtypeStruct((1, TOKENS, FEATURE...  67.5 us
    pallas_call x1, Pallas kernels, per_device(): pl.pallas_call(place, out_shape=jax.ShapeDtypeStruct((1, TOKENS, FEATURES...  1.91 us

profile of v4, /device:TPU:1, one launch (start us, length us, event | category | flops | bytes accessed | tf_op | source)
XLA Modules:
  0.0 69.4 jit_solution(17880848772483335199)
XLA Ops:
  0.0 67.5 %project_attend.1.source = bf16[1,128,3072]{2,1,0:T(8,128)(2,1)} custom-call(bf16[1,128,3072]{2,1,0:T(8,128)(2,1)} %patches.1, s32[384,3072]{1,0:T(8,128)} %codes.1, f32[3,24]{1,0:T(4,128)} %scales.1, bf16[1,128,3072]{2,1,0:T(8,128)(2,1)} %keys.1, bf16[1,128,3072]{2,1,0:T(8,128)(2,1)} %values.1, f32[1,3072]{1,0:T(1,128)} %bitcast.2, f32[1,3072]{1,0:T(1,128)} %bitcast.3), custom_call_target="tpu_custom_call" | custom-call | tf_op jit(solution)/shard_map/project_attend/pallas_call | solution.py:454
  67.5 1.9 %place.1 = bf16[1,128,3072]{2,1,0:T(8,128)(2,1)} custom-call(bf16[1,128,3072]{2,1,0:T(8,128)(2,1)} %project_attend.1.source), custom_call_target="tpu_custom_call" | custom-call | tf_op jit(solution)/shard_map/place/pallas_call | solution.py:489
